TPU v7x, 32 devices: a whole 2x2x4 slice. The times are simulated.
32 devices in a mesh: front: 4 (over y, core), blk: 8 (over z, x).
Axes of the slice: x: 2, y: 2, z: 4, core: 2. Of those that a mesh axis runs over, the one named last changes fastest.
Arguments:
- front: float32 [4, 1024, 1024], P('front', 'blk'), parts along dimension 0, may hold values from -8 to 40, as said below
- child: float32 [4, 512, 512], P('front', 'blk'), parts along dimension 0, may hold values from -1 to 4, as said below
- index_map: int32 [2048], P('front'), parts along dimension 0, may hold values from 0 to 1023, as said below
Outputs:
- factored: float32 [4, 1024, 1024], P('front', 'blk'), parts along dimension 0
There are 4 independent parts, one for each index of `front`. A program takes and returns all parts, laid end to end along the dimension named above; each array names one. Nothing has to cross between parts.
Inputs may be any that keep to these rules, and one draw needn't show every extreme that they name: front is symmetric and positive definite. child is symmetric and positive semidefinite. `index_map`: tile t of the child (indices t * 64 to t * 64 + 63, with t = k * 8 + e and e < 8) maps in increasing order onto 64 different indices of the front's block column b = k * 8 + ((e + h) mod 8), where h is half of 8, that is onto indices b * 128 to b * 128 + 127; no two child indices share a front index.
All inputs are finite; a program needn't handle non-finite values.
Results may differ from a plain program's by a relative error of at most 0.0034.
Values may be sent and summed in bfloat16 or wider, within the bound.
No kernel may reach another device: no remote copies, remote signals or barrier semaphores. Data moves between devices by JAX's collectives and lax.ppermute only.
A program may use at most 128 MiB of HBM per device.

v0:
```python
import jax
import jax.numpy as jnp
from jax import lax
from jax.experimental import pallas as pl
from jax.experimental.pallas import tpu as pltpu
from jax.sharding import PartitionSpec as P


PANEL_WIDTH = 512
BLOCK_WIDTH = 128
COL_BLOCKS = 1
TILE_WIDTH = 64


HIGHEST = lax.Precision.HIGHEST


F32 = jnp.float32
BF16 = jnp.bfloat16
LANES = 128
SUBS = 8
WIDTH = 2
GROUP = 16
KERNEL_BYTES = 16 * 1024 * 1024


def lane_copy(tile, lane):
    return jnp.broadcast_to(tile[:, lane:lane+1], tile.shape)


def row_copy(tile, row):
    return jnp.broadcast_to(tile[row:row+1, :], tile.shape)


def tree_sum(terms):
    while len(terms) > 1:
        terms = [a + b for a, b in zip(terms[::2], terms[1::2])] + ([terms[-1]] if len(terms) % 2 else [])
    return terms[0]


def halves(x):
    high = x.astype(BF16)
    return high, (x - high.astype(F32)).astype(BF16)


def product3(left, right):
    (lh, ll), (rh, rl) = left, right
    mm = lambda x, y: jnp.dot(x, y, preferred_element_type=F32)
    return mm(lh, rh) + (mm(lh, rl) + mm(ll, rh))


def eliminate(tiles, start_lane, zero):
    count = len(tiles)
    tiles = list(tiles)
    shape = (SUBS, LANES)
    lane = lax.broadcasted_iota(jnp.int32, shape, 1)
    sub = lax.broadcasted_iota(jnp.int32, shape, 0)
    at_row = [sub == k for k in range(SUBS)]
    unit = [jnp.where(at, 1.0, 0.0) for at in at_row]
    results = []
    own = range(WIDTH)
    span = WIDTH * SUBS
    for head in range(0, count, WIDTH):
        first = start_lane + head * SUBS
        inside = (lane >= first) & (lane < first + span)
        cols = [[None] * span for _ in own]
        for m in range(span):
            for t in own:
                cols[t][m] = lane_copy(tiles[head + t], first + m) + (zero if t == 0 else 0.0)
        later = {}
        for m in range(span):
            for i in range(head + WIDTH, count):
                later[i, m] = lane_copy(tiles[i], first + m)
        joined = [
            jnp.where(inside, jnp.where(lane - (first + t * SUBS) == sub, 1.0, 0.0), tiles[head + t]) for t in own
        ]
        result = [jnp.zeros(shape, F32) for _ in own]
        for k in range(span):
            at, r = divmod(k, SUBS)
            root = lax.rsqrt(row_copy(cols[at][k], r))
            inv = root * root
            weight = [cols[t][k] - unit[r] if t == at else cols[t][k] for t in own]
            for m in range(k + 1, span):
                pivot = row_copy(cols[at][m], r)
                if m == k + 1:
                    for t in own:
                        cols[t][m] = cols[t][m] - (weight[t] * pivot) * inv
                else:
                    pivot = pivot * inv
                    for t in own:
                        cols[t][m] = cols[t][m] - weight[t] * pivot
            pivot = row_copy(joined[at], r)
            result[at] = jnp.where(at_row[r], pivot * root, result[at])
            pivot = pivot * inv
            for t in own:
                joined[t] = joined[t] - weight[t] * pivot
        results += result
        rows = [row_copy(joined[k // SUBS], k % SUBS) for k in range(span)]
        for i in range(head + WIDTH, count):
            update = tree_sum([later[i, k] * rows[k] for k in range(span)])
            tiles[i] = jnp.where(inside, 0.0, tiles[i]) - update
    return results


def inverse_tiles(tiles, zero):
    tiles = list(tiles)
    lane = lax.broadcasted_iota(jnp.int32, (SUBS, LANES), 1)
    sub = lax.broadcasted_iota(jnp.int32, (SUBS, LANES), 0)
    inverses = []
    for g in range(0, len(tiles), GROUP):
        results = eliminate(tiles[g : g + GROUP], g * SUBS, zero)
        kept = [jnp.where(lane <= (g + t) * SUBS + sub, result, 0.0) for t, result in enumerate(results)]
        inverses += kept
        done = (g + GROUP) * SUBS
        if done < BLOCK_WIDTH:
            scaled = jnp.concatenate(
                [jnp.where(lane < done, low, result) for low, result in zip(kept, results)], axis=0
            )
            update = product3(halves(scaled.T[done:, :]), halves(scaled))
            group_lanes = (lane >= g * SUBS) & (lane < done)
            for t in range(g + GROUP, len(tiles)):
                at = t * SUBS - done
                tiles[t] = jnp.where(group_lanes, 0.0, tiles[t]) - update[at : at + SUBS, :]
    return inverses


def block_rows(b):
    return pl.ds(pl.multiple_of(b * BLOCK_WIDTH, BLOCK_WIDTH), BLOCK_WIDTH)


def block_lanes(j):
    return slice(j * BLOCK_WIDTH, (j + 1) * BLOCK_WIDTH)


def exact_parts(values):
    parts = []
    for _ in range(3):
        parts.append(values.astype(BF16))
        values = values - parts[-1].astype(F32)
    return parts


def place_columns(part, col_hot, q):
    pair = 2 * TILE_WIDTH
    return jnp.dot(
        part[:, q * pair : (q + 1) * pair], col_hot[q * pair : (q + 1) * pair, :], preferred_element_type=F32
    )


def lay_square(me, slabs, square):
    count = len(slabs)
    for m in range(count):
        owner = jnp.bitwise_xor(me, m)
        for step in range(slabs[m].shape[1] // BLOCK_WIDTH):
            square[(owner + step) % count, block_rows(owner), :] = slabs[m][:, block_lanes(step)]
    square[count - 1, :BLOCK_WIDTH, :] = square[0, (count - 1) * BLOCK_WIDTH : count * BLOCK_WIDTH, :].T
    across = count // 2

    @pl.when(me >= across)
    def _():
        for b in range(across):
            square[b + across, block_lanes(b), :] = square[b, block_lanes(b + across), :].T


def factor_panel(square, inverse, zero):
    count = square.shape[0]
    above = lax.broadcasted_iota(jnp.int32, (BLOCK_WIDTH, BLOCK_WIDTH), 0) <= lax.broadcasted_iota(
        jnp.int32, (BLOCK_WIDTH, BLOCK_WIDTH), 1
    )
    for b in range(count):
        base = b * BLOCK_WIDTH
        rows = slice(base, base + BLOCK_WIDTH)
        tiles = [square[b, base + SUBS * t : base + SUBS * (t + 1), :] for t in range(BLOCK_WIDTH // SUBS)]
        own_inverse = jnp.concatenate(inverse_tiles(tiles, zero), axis=0)
        inverse[rows, :] = own_inverse
        scale = halves(own_inverse)
        lefts = {}
        for j in range(b + 1, count):
            value = product3(scale, halves(square[j, rows, :]))
            square[j, rows, :] = value
            right = halves(value)
            lefts[j] = halves(value.T)
            for i in range(b + 1, j + 1):
                square[j, i * BLOCK_WIDTH : (i + 1) * BLOCK_WIDTH, :] -= product3(lefts[i], right)
        square[b, rows, :] = jnp.where(above, product3(scale, halves(square[b, rows, :])), 0.0)


def spread_rows(kids, row_hot, col_hot, full):
    pair = 2 * TILE_WIDTH
    pairs = kids.shape[1] // pair
    parts = [
        jnp.dot(row_hot[...], part, preferred_element_type=F32).astype(BF16) for part in exact_parts(kids[...])
    ]
    for q in range(pairs):
        total = sum(place_columns(part, col_hot, (q + pairs // 2) % pairs) for part in parts)
        for which in range(2):
            full[2 * q + which] = total[:, which * BLOCK_WIDTH : (which + 1) * BLOCK_WIDTH]


def rows_kernel(where, slab, kids, row_hot, col_hot, diag, wide_diag, side, full):
    count = PANEL_WIDTH // BLOCK_WIDTH
    me, half = where[0], where[1]
    spread_rows(kids, row_hot, col_hot, full)
    for j in range(2 * count):
        full[j] += slab[:, block_lanes(j)]
    for step in range(count - 1):
        wide_diag[:, block_lanes(step)] = full[half * count + (me + step) % count]
    diag[...] = wide_diag[:, : diag.shape[1]]
    for j in range(count):
        side[:, block_lanes(j)] = full[(1 - half) * count + j]


def far_kernel(where, raw, kids, row_hot, col_hot, out, wide_out, full):
    count = PANEL_WIDTH // BLOCK_WIDTH
    me, half = where[0], where[1]
    spread_rows(kids, row_hot, col_hot, full)
    for step in range(count - 1):
        wide_out[:, block_lanes(step)] = raw[:, block_lanes(step)] + full[(1 - half) * count + (me + step) % count]
    out[...] = wide_out[:, : out.shape[1]]


def first_kernel(where, *refs):
    count = PANEL_WIDTH // BLOCK_WIDTH
    slabs, (upper, inverse) = refs[:count], refs[count:]
    lay_square(where[0], slabs, upper)
    factor_panel(upper, inverse, slabs[0][:SUBS, :LANES] * 0.0)


def second_kernel(where, *refs):
    count = PANEL_WIDTH // BLOCK_WIDTH
    sides, fars = refs[:count], refs[count : 2 * count]
    upper, inverse, mine, send, side, square, own_inverse = refs[2 * count :]
    me, half = where[0], where[1]
    for m in range(count):
        side[block_rows(jnp.bitwise_xor(me, m)), :] = sides[m][...]
    lay_square(me, fars, square)
    for b in range(count):
        rows = slice(b * BLOCK_WIDTH, (b + 1) * BLOCK_WIDTH)
        value = product3(halves(inverse[rows, :]), halves(side[rows, :]))
        side[rows, :] = value
        solved = halves(value)
        for i in range(b + 1, count):
            side[i * BLOCK_WIDTH : (i + 1) * BLOCK_WIDTH, :] -= product3(halves(upper[i, rows, :].T), solved)
    rounded = side[...].astype(BF16)
    for i in range(count):
        left = rounded[:, i * BLOCK_WIDTH : (i + 1) * BLOCK_WIDTH].T
        total = jnp.dot(left, rounded[:, i * BLOCK_WIDTH :], preferred_element_type=F32)
        for j in range(i, count):
            square[j, i * BLOCK_WIDTH : (i + 1) * BLOCK_WIDTH, :] -= total[
                :, (j - i) * BLOCK_WIDTH : (j - i + 1) * BLOCK_WIDTH
            ]
    factor_panel(square, own_inverse, sides[0][:SUBS, :LANES] * 0.0)
    rows = block_rows(me)
    for j in range(count):
        kept = (j >= me) & (half == 0)
        mine[:, block_lanes(j)] = jnp.where(kept, upper[j, rows, :], 0.0).astype(BF16).astype(F32)
        send[:, block_lanes(j)] = jnp.where(j >= me, square[j, rows, :], 0.0).astype(BF16)
    mine[:, PANEL_WIDTH:] = side[rows, :].astype(BF16).astype(F32)


def finish_kernel(where, mine, got, out, done):
    @pl.when(where[1] == 1)
    def _():
        mine[:, PANEL_WIDTH:] = got[...].astype(F32)

    copy = pltpu.make_async_copy(mine, out, done)
    copy.start()
    copy.wait()


def two_panels(front, child, index_map):
    cycle_size = lax.axis_size("blk")
    my_index = lax.axis_index("blk")
    count = PANEL_WIDTH // BLOCK_WIDTH
    me = my_index % count
    half = my_index // count

    def swap(shard, by):
        return lax.ppermute(shard, "blk", [(i, i ^ by) for i in range(cycle_size)])

    def share(shard, wide):
        return [wide] + [swap(wide if m == 1 else shard, m) for m in range(1, count)]

    def row_hot(block):
        own = lax.dynamic_slice_in_dim(places, block * TILE_WIDTH, TILE_WIDTH)
        return (jnp.arange(BLOCK_WIDTH, dtype=jnp.int32)[:, None] == own).astype(BF16)

    places = index_map % BLOCK_WIDTH
    tiles = jnp.arange(places.shape[0], dtype=jnp.int32) // TILE_WIDTH
    col_hot = ((places + tiles % 2 * BLOCK_WIDTH)[:, None] == jnp.arange(2 * BLOCK_WIDTH, dtype=jnp.int32)).astype(BF16)

    scalar = pl.BlockSpec(memory_space=pltpu.SMEM)
    vector = pl.BlockSpec(memory_space=pltpu.VMEM)
    where = jnp.stack([me, half]).astype(jnp.int32)
    square_shape = (count, PANEL_WIDTH, BLOCK_WIDTH)
    inverse_shape = (PANEL_WIDTH, BLOCK_WIDTH)
    diag_shape = (BLOCK_WIDTH, (count - 2) * BLOCK_WIDTH)
    wide_shape = (BLOCK_WIDTH, (count - 1) * BLOCK_WIDTH)
    side_shape = (BLOCK_WIDTH, PANEL_WIDTH)
    full = pltpu.VMEM((cycle_size, BLOCK_WIDTH, BLOCK_WIDTH), F32)

    grant = pltpu.CompilerParams(vmem_limit_bytes=KERNEL_BYTES)

    def near(array):
        return pltpu.with_memory_space_constraint(array, pltpu.VMEM)

    def local(kernel, outs, ins, scratch=()):
        return pl.pallas_call(
            kernel,
            out_shape=[pltpu.VMEM(*out) for out in outs],
            in_specs=[scalar] + [vector] * len(ins),
            out_specs=[vector] * len(outs),
            scratch_shapes=scratch,
            compiler_params=grant,
        )(where, *[near(array) for array in ins])

    slab, kids = front[0], child[0]
    arrived = swap(kids, count)
    raw = jnp.concatenate(
        [
            lax.dynamic_slice_in_dim(slab, (half * count + (me + step) % count) * BLOCK_WIDTH, BLOCK_WIDTH, 1)
            for step in range(count - 1)
        ],
        axis=1,
    )
    far = swap(raw, count)
    own_hot, far_hot = row_hot((my_index + count) % cycle_size), row_hot(my_index)
    diag, wide_diag, side = local(
        rows_kernel,
        [(diag_shape, F32), (wide_shape, F32), (side_shape, F32)],
        [slab, arrived, own_hot, col_hot],
        [full],
    )
    diags = share(diag, wide_diag)
    sides = share(side, side)
    far, wide_far = local(far_kernel, [(diag_shape, F32), (wide_shape, F32)], [far, kids, far_hot, col_hot], [full])
    fars = share(far, wide_far)
    upper, inverse = local(first_kernel, [(square_shape, F32), (inverse_shape, F32)], diags)
    mine, send = local(
        second_kernel,
        [((BLOCK_WIDTH, 2 * PANEL_WIDTH), F32), (side_shape, BF16)],
        [*sides, *fars, upper, inverse],
        [
            pltpu.VMEM((PANEL_WIDTH, PANEL_WIDTH), F32),
            pltpu.VMEM(square_shape, F32),
            pltpu.VMEM(inverse_shape, F32),
        ],
    )
    got = swap(send, count)
    result = pl.pallas_call(
        finish_kernel,
        out_shape=jax.ShapeDtypeStruct((BLOCK_WIDTH, 2 * PANEL_WIDTH), F32),
        in_specs=[scalar, vector, vector],
        out_specs=pl.BlockSpec(memory_space=pl.ANY),
        scratch_shapes=[pltpu.SemaphoreType.DMA],
        compiler_params=grant,
        name="finish",
    )(where, near(mine), near(got))
    return result[None]


def is_two_panels(cycle_size):
    return COL_BLOCKS == 1 and cycle_size * BLOCK_WIDTH == 2 * PANEL_WIDTH


def on_device(front, child, index_map):
    if is_two_panels(lax.axis_size("blk")):
        return two_panels(front, child, index_map)
    return any_cycle(front, child, index_map)


def from_behind(shard, axis, by):
    count = lax.axis_size(axis)
    return lax.ppermute(shard, axis, [(i, (i + by) % count) for i in range(count)])


def column_numbers(cycle_size, my_index):
    local_ids = jnp.arange(COL_BLOCKS * BLOCK_WIDTH, dtype=jnp.int32)
    return (
        local_ids // BLOCK_WIDTH * cycle_size + my_index
    ) * BLOCK_WIDTH + local_ids % BLOCK_WIDTH


def row_numbers(cycle_size):
    stored = jnp.arange(cycle_size * COL_BLOCKS * BLOCK_WIDTH, dtype=jnp.int32)
    holder = stored // (COL_BLOCKS * BLOCK_WIDTH)
    within = stored // BLOCK_WIDTH % COL_BLOCKS
    return (within * cycle_size + holder) * BLOCK_WIDTH + stored % BLOCK_WIDTH


def cycle_rows(matrix, cycle_size):
    height = matrix.shape[0]
    return (
        matrix.reshape(height, COL_BLOCKS, cycle_size, BLOCK_WIDTH)
        .transpose(0, 2, 1, 3)
        .reshape(height, -1)
    )


def natural_rows(matrix, cycle_size):
    height = matrix.shape[0]
    return (
        matrix.reshape(height, cycle_size, COL_BLOCKS, BLOCK_WIDTH)
        .transpose(0, 2, 1, 3)
        .reshape(height, -1)
    )


def panel_rows(matrix, row_start, cycle_size):
    first_owner = row_start // BLOCK_WIDTH
    owner_count = PANEL_WIDTH // BLOCK_WIDTH
    height = matrix.shape[0]
    blocks = matrix.reshape(height, cycle_size, COL_BLOCKS, BLOCK_WIDTH)
    return blocks[:, first_owner : first_owner + owner_count, 0, :].reshape(height, PANEL_WIDTH)


def ownership(row_start, my_index):
    first_owner = row_start // BLOCK_WIDTH
    owner_count = PANEL_WIDTH // BLOCK_WIDTH
    is_owner = (my_index >= first_owner) & (my_index < first_owner + owner_count)
    column_start = jnp.clip(my_index - first_owner, 0, owner_count - 1) * BLOCK_WIDTH
    return (is_owner, column_start)


def collect(stacked, row_start, my_index):
    is_owner, column_start = ownership(row_start, my_index)
    padded = jnp.zeros((stacked.shape[0], PANEL_WIDTH, PANEL_WIDTH), jnp.float32)
    padded = lax.dynamic_update_slice(
        padded, jnp.where(is_owner, stacked, 0.0), (0, column_start, 0)
    )
    result = lax.psum(padded, "blk")
    return result


def own_rows(diag_factor, panel_part, row_start, columns):
    solved = lax.linalg.triangular_solve(
        diag_factor, panel_part, left_side=False, lower=True, transpose_a=True
    )
    offsets = columns - row_start
    diag_rows = jnp.take(diag_factor, jnp.clip(offsets, 0, PANEL_WIDTH - 1), axis=0)
    inside = (offsets >= 0) & (offsets < PANEL_WIDTH)
    before = offsets < 0
    return jnp.where(inside[:, None], diag_rows, jnp.where(before[:, None], 0.0, solved))


def make_refresh(working, lowered, owned_panels):

    def refresh(received, offset):
        updated = working - lax.dot_general(
            lowered, received, (((1,), (1,)), ((), ())), preferred_element_type=jnp.float32
        )
        leading = updated
        for is_owner, column_start in owned_panels:
            factor_column = (
                lax.dynamic_slice_in_dim(received, column_start, BLOCK_WIDTH, 1)
                .astype(jnp.float32)
                .T
            )
            leading = jnp.where(is_owner, factor_column, leading)
        return jnp.concatenate([leading, updated[BLOCK_WIDTH:]], axis=0)

    return refresh


def assemble(front, child, index_map, cycle_size, my_index):
    half_cycle = cycle_size // 2
    arrived_tiles = from_behind(child, "blk", half_cycle)
    full_order = 2 * index_map.shape[0]
    tile_places = (index_map % BLOCK_WIDTH).reshape(COL_BLOCKS, cycle_size, TILE_WIDTH)
    places = jnp.arange(BLOCK_WIDTH, dtype=jnp.int32)
    row_table = (tile_places[..., None] == places).astype(jnp.float32)
    shaped = arrived_tiles.reshape(COL_BLOCKS, TILE_WIDTH, COL_BLOCKS, cycle_size, TILE_WIDTH)
    spread = jnp.einsum("acbei,beiq->acbeq", shaped, row_table, precision=HIGHEST)
    spread = jnp.roll(spread, half_cycle, axis=3).reshape(COL_BLOCKS, TILE_WIDTH, full_order)
    source = (my_index - half_cycle) % cycle_size
    own_places = lax.dynamic_index_in_dim(tile_places, source, axis=1, keepdims=False)
    column_table = (own_places[..., None] == places).astype(jnp.float32)
    placed = jnp.einsum("kcq,kcn->kqn", column_table, spread, precision=HIGHEST)
    return front + placed


def any_cycle(front, child, index_map):
    cycle_size = lax.axis_size("blk")
    my_index = lax.axis_index("blk")
    local_width = COL_BLOCKS * BLOCK_WIDTH
    assembled = assemble(front, child, index_map, cycle_size, my_index).reshape(local_width, -1)
    working = cycle_rows(assembled, cycle_size)
    columns = column_numbers(cycle_size, my_index)
    for row_start in (0, PANEL_WIDTH):
        panel_part = panel_rows(working, row_start, cycle_size)
        diag_block = collect(panel_part[None, :BLOCK_WIDTH], row_start, my_index)[0]
        lowered = own_rows(jnp.linalg.cholesky(diag_block), panel_part, row_start, columns).astype(
            jnp.bfloat16
        )
        refresh = make_refresh(working, lowered, (ownership(row_start, my_index),))
        working = refresh(lax.all_gather(lowered, "blk", axis=0, tiled=True), jnp.int32(0))
    trailing = columns >= 2 * PANEL_WIDTH
    leading_rows = row_numbers(cycle_size) < 2 * PANEL_WIDTH
    working = jnp.where(trailing[:, None] & leading_rows[None, :], 0.0, working)
    return natural_rows(working, cycle_size).reshape(COL_BLOCKS, BLOCK_WIDTH, -1)


def solution(mesh):
    placed = (P("front", "blk", None), P("front", "blk", None), P("front"))
    return jax.shard_map(
        on_device, mesh=mesh, in_specs=placed, out_specs=P("front", "blk", None), check_vma=False
    )
```

profile of v0, /device:TPU:0, one launch (start us, length us, event | category | flops | bytes accessed | tf_op | source)
XLA Modules:
  0.0 73.6 jit_solution(14406958730380248921)
XLA Ops:
  0.0 4.1 %collective-permute-start = (f32[64,512]{1,0:T(8,128)}, f32[64,512]{1,0:T(8,128)S(1)}, u32[]{:S(2)}, u32[]{:S(2)}) collective-permute-start(f32[64,512]{1,0:T(8,128)} %bitcast.12), channel_id=1, source_target_pairs={{0,4},{1,5},{2,6},{3,7},{4,0},{5,1},{6,2},{7,3},{8,12},{9,13},{10,... | collective-permute-start | bytes 393224 | tf_op jit(solution)/shard_map/ppermute | solution.py:279
  4.1 1.0 %dynamic-slice_bitcast_fusion.2 = (f32[128,128]{1,0:T(8,128)S(1)}, f32[128,128]{1,0:T(8,128)S(1)}, f32[128,128]{1,0:T(8,128)S(1)}) fusion(f32[1,128,1024]{2,1,0:T(8,128)} %param.3, s32[]{:T(128)S(6)} %select_n.65, s32[]{:T(128)S(6)} %select_n.69, s32[]{:T(128)S(6)} %select_n.67), kind=kLoop, calls=%fused_computation.6 | loop fusion | bytes 393228 | tf_op jit(solution)/shard_map/dynamic_slice | solution.py:321
  5.2 0.7 copy-done.2
  5.9 0.1 fusion.col_hot
  6.2 9.5 %collective-permute-done.kids = f32[64,512]{1,0:T(8,128)S(1)} collective-permute-done((f32[64,512]{1,0:T(8,128)}, f32[64,512]{1,0:T(8,128)S(1)}, u32[]{:S(2)}, u32[]{:S(2)}) %collective-permute-start) | collective-permute-done | bytes 131104 | tf_op jit(solution)/shard_map/ppermute | solution.py:279
  15.6 1.1 %shard_map.37 = (f32[128,256]{1,0:T(8,128)S(1)}, f32[128,384]{1,0:T(8,128)S(1)}, f32[128,512]{1,0:T(8,128)S(1)}) custom-call(s32[2]{0:T(128)S(1)} %pad_add_fusion.where, f32[128,1024]{1,0:T(8,128)S(1)} %bitcast.11, f32[64,512]{1,0:T(8,128)S(1)} %collective-permute-done.kids, bf16[128,64]{1,0:T(8,128)(2,1)S(1)} %fusion.1.row_hot, ...), custom_call_target="tpu_custom_call" | custom-call | tf_op jit(solution)/shard_map/pallas_call | solution.py:308
  16.8 1.1 %collective-permute-start.10 = (f32[128,256]{1,0:T(8,128)S(1)}, f32[128,256]{1,0:T(8,128)S(1)}, u32[]{:S(2)}, u32[]{:S(2)}) collective-permute-start(f32[128,256]{1,0:T(8,128)S(1)} %get-tuple-element.18), channel_id=1, source_target_pairs={{0,3},{1,2},{2,1},{3,0},{4,7},{5,6},{6,5},{7,4},{8,11},{9,10},{10,... | collective-permute-start | bytes 393224 | tf_op jit(solution)/shard_map/ppermute | solution.py:279
  17.8 2.3 %collective-permute-start.9 = (f32[128,256]{1,0:T(8,128)S(1)}, f32[128,256]{1,0:T(8,128)S(1)}, u32[]{:S(2)}, u32[]{:S(2)}) collective-permute-start(f32[128,256]{1,0:T(8,128)S(1)} %get-tuple-element.18), channel_id=1, source_target_pairs={{0,2},{1,3},{2,0},{3,1},{4,6},{5,7},{6,4},{7,5},{8,10},{9,11},{10,... | collective-permute-start | bytes 393224 | tf_op jit(solution)/shard_map/ppermute | solution.py:279
  20.1 0.3 collective-permute-start.8
  20.4 1.1 %shard_map.38 = (f32[128,256]{1,0:T(8,128)S(1)}, f32[128,384]{1,0:T(8,128)S(1)}) custom-call(s32[2]{0:T(128)S(1)} %pad_add_fusion.where, f32[128,384]{1,0:T(8,128)S(1)} %collective-permute-done.4.raw, f32[64,512]{1,0:T(8,128)S(1)} %bitcast.13, bf16[128,64]{1,0:T(8,128)(2,1)S(1)} %fusion.2.row_hot, bf16[512,256]{1,0:T(8,128)(2,1)S(1)} %fusion.col_hot), custom_call_target="tpu_custom_call" | custom-call | tf_op jit(solution)/shard_map/pallas_call | solution.py:308
  21.5 1.3 %collective-permute-start.7 = (f32[128,256]{1,0:T(8,128)S(1)}, f32[128,256]{1,0:T(8,128)S(1)}, u32[]{:S(2)}, u32[]{:S(2)}) collective-permute-start(f32[128,256]{1,0:T(8,128)S(1)} %get-tuple-element.16), channel_id=1, source_target_pairs={{0,3},{1,2},{2,1},{3,0},{4,7},{5,6},{6,5},{7,4},{8,11},{9,10},{10,... | collective-permute-start | bytes 393224 | tf_op jit(solution)/shard_map/ppermute | solution.py:279
  22.8 1.7 %collective-permute-start.3 = (f32[128,512]{1,0:T(8,128)S(1)}, f32[128,512]{1,0:T(8,128)S(1)}, u32[]{:S(2)}, u32[]{:S(2)}) collective-permute-start(f32[128,512]{1,0:T(8,128)S(1)} %get-tuple-element.14.refs_0_), channel_id=1, source_target_pairs={{0,3},{1,2},{2,1},{3,0},{4,7},{5,6},{6,5},{7,4},{8,11},{9,10},{10,... | collective-permute-start | bytes 786440 | tf_op jit(solution)/shard_map/ppermute | solution.py:279
  24.5 0.4 collective-permute-start.2
  24.9 1.7 %collective-permute-done.9.refs_2_ = f32[128,256]{1,0:T(8,128)S(1)} collective-permute-done((f32[128,256]{1,0:T(8,128)S(1)}, f32[128,256]{1,0:T(8,128)S(1)}, u32[]{:S(2)}, u32[]{:S(2)}) %collective-permute-start.9) | collective-permute-done | bytes 131104 | tf_op jit(solution)/shard_map/ppermute | solution.py:279
  26.5 0.9 %collective-permute-start.1 = (f32[128,512]{1,0:T(8,128)S(1)}, f32[128,512]{1,0:T(8,128)S(1)}, u32[]{:S(2)}, u32[]{:S(2)}) collective-permute-start(f32[128,512]{1,0:T(8,128)S(1)} %get-tuple-element.14.refs_0_), channel_id=1, source_target_pairs={{0,1},{1,0},{2,3},{3,2},{4,5},{5,4},{6,7},{7,6},{8,9},{9,8},{10,11... | collective-permute-start | bytes 786440 | tf_op jit(solution)/shard_map/ppermute | solution.py:279
  27.5 2.2 %collective-permute-done.7.refs_7_ = f32[128,256]{1,0:T(8,128)S(1)} collective-permute-done((f32[128,256]{1,0:T(8,128)S(1)}, f32[128,256]{1,0:T(8,128)S(1)}, u32[]{:S(2)}, u32[]{:S(2)}) %collective-permute-start.7) | collective-permute-done | bytes 131104 | tf_op jit(solution)/shard_map/ppermute | solution.py:279
  29.7 1.1 %collective-permute-start.5 = (f32[128,384]{1,0:T(8,128)S(1)}, f32[128,384]{1,0:T(8,128)S(1)}, u32[]{:S(2)}, u32[]{:S(2)}) collective-permute-start(f32[128,384]{1,0:T(8,128)S(1)} %get-tuple-element.15.refs_4_), channel_id=1, source_target_pairs={{0,1},{1,0},{2,3},{3,2},{4,5},{5,4},{6,7},{7,6},{8,9},{9,8},{10,11... | collective-permute-start | bytes 589832 | tf_op jit(solution)/shard_map/ppermute | solution.py:279
  30.8 5.7 %collective-permute-done.8.refs_1_ = f32[128,384]{1,0:T(8,128)S(1)} collective-permute-done((f32[128,384]{1,0:T(8,128)S(1)}, f32[128,384]{1,0:T(8,128)S(1)}, u32[]{:S(2)}, u32[]{:S(2)}) %collective-permute-start.8) | collective-permute-done | bytes 196640 | tf_op jit(solution)/shard_map/ppermute | solution.py:279
  36.5 0.2 collective-permute-start.6
  36.7 12.2 %shard_map.39 = (f32[4,512,128]{2,1,0:T(8,128)S(1)}, f32[512,128]{1,0:T(8,128)S(1)}) custom-call(s32[2]{0:T(128)S(1)} %pad_add_fusion.where, f32[128,384]{1,0:T(8,128)S(1)} %get-tuple-element.17.refs_0_, f32[128,384]{1,0:T(8,128)S(1)} %collective-permute-done.8.refs_1_, f32[128,256]{1,0:T(8,128)S(1)} %collective-permute-done.9.refs_2_, ...), custom_call_target="tpu_custom_call" | custom-call | tf_op jit(solution)/shard_map/pallas_call | solution.py:308
  48.9 14.5 %shard_map.40 = (f32[128,1024]{1,0:T(8,128)S(1)}, bf16[128,512]{1,0:T(8,128)(2,1)S(1)}) custom-call(s32[2]{0:T(128)S(1)} %pad_add_fusion.where, f32[128,512]{1,0:T(8,128)S(1)} %get-tuple-element.14.refs_0_, f32[128,512]{1,0:T(8,128)S(1)} %collective-permute-done.1.refs_1_, f32[128,512]{1,0:T(8,128)S(1)} %collective-permute-done.2.refs_2_, ...), custom_call_target="tpu_custom_call" | custom-call | tf_op jit(solution)/shard_map/pallas_call | solution.py:308
  63.4 3.1 %collective-permute-start.11 = (bf16[128,512]{1,0:T(8,128)(2,1)S(1)}, bf16[128,512]{1,0:T(8,128)(2,1)S(1)}, u32[]{:S(2)}, u32[]{:S(2)}) collective-permute-start(bf16[128,512]{1,0:T(8,128)(2,1)S(1)} %get-tuple-element.22), channel_id=1, source_target_pairs={{0,4},{1,5},{2,6},{3,7},{4,0},{5,1},{6,2},{7,3},{8,12},{9,13},{10,... | collective-permute-start | bytes 393224 | tf_op jit(solution)/shard_map/ppermute | solution.py:279
  66.5 5.6 %collective-permute-done.11.got = bf16[128,512]{1,0:T(8,128)(2,1)S(1)} collective-permute-done((bf16[128,512]{1,0:T(8,128)(2,1)S(1)}, bf16[128,512]{1,0:T(8,128)(2,1)S(1)}, u32[]{:S(2)}, u32[]{:S(2)}) %collective-permute-start.11) | collective-permute-done | bytes 131104 | tf_op jit(solution)/shard_map/ppermute | solution.py:279
  72.1 1.3 %finish.1 = f32[128,1024]{1,0:T(8,128)} custom-call(s32[2]{0:T(128)S(1)} %pad_add_fusion.where, f32[128,1024]{1,0:T(8,128)S(1)} %get-tuple-element.21.mine, bf16[128,512]{1,0:T(8,128)(2,1)S(1)} %collective-permute-done.11.got), custom_call_target="tpu_custom_call" | custom-call | tf_op jit(solution)/shard_map/finish/pallas_call | solution.py:350
  (19 shorter events, 0.3 us)
Async XLA Ops:
  0.0 15.6 %collective-permute-start = (f32[64,512]{1,0:T(8,128)}, f32[64,512]{1,0:T(8,128)S(1)}, u32[]{:S(2)}, u32[]{:S(2)}) collective-permute-start(f32[64,512]{1,0:T(8,128)} %bitcast.12), channel_id=1, source_target_pairs={{0,4},{1,5},{2,6},{3,7},{4,0},{5,1},{6,2},{7,3},{8,12},{9,13},{10,... | collective-permute-start | bytes 393224 | tf_op jit(solution)/shard_map/ppermute | solution.py:279
  4.1 11.6 %copy-start = (f32[1,128,1024]{2,1,0:T(8,128)S(1)}, f32[1,128,1024]{2,1,0:T(8,128)}, u32[]{:S(2)}) copy-start(f32[1,128,1024]{2,1,0:T(8,128)} %param.3) | copy-start | bytes 1572868
  5.1 15.3 %collective-permute-start.4 = (f32[128,384]{1,0:T(8,128)S(1)}, f32[128,384]{1,0:T(8,128)S(1)}, u32[]{:S(2)}, u32[]{:S(2)}) collective-permute-start(f32[128,384]{1,0:T(8,128)S(1)} %pad_maximum_fusion), channel_id=1, source_target_pairs={{0,4},{1,5},{2,6},{3,7},{4,0},{5,1},{6,2},{7,3},{8,12},{9,13},{10,... | collective-permute-start | bytes 589832 | tf_op jit(solution)/shard_map/ppermute | solution.py:279
  5.2 0.7 copy-start.2
  15.6 4.8 %copy-start.1 = (f32[1,64,512]{2,1,0:T(8,128)S(1)}, f32[1,64,512]{2,1,0:T(8,128)}, u32[]{:S(2)}) copy-start(f32[1,64,512]{2,1,0:T(8,128)} %param.4) | copy-start | bytes 393220
  16.8 7.7 %collective-permute-start.10 = (f32[128,256]{1,0:T(8,128)S(1)}, f32[128,256]{1,0:T(8,128)S(1)}, u32[]{:S(2)}, u32[]{:S(2)}) collective-permute-start(f32[128,256]{1,0:T(8,128)S(1)} %get-tuple-element.18), channel_id=1, source_target_pairs={{0,3},{1,2},{2,1},{3,0},{4,7},{5,6},{6,5},{7,4},{8,11},{9,10},{10,... | collective-permute-start | bytes 393224 | tf_op jit(solution)/shard_map/ppermute | solution.py:279
  17.8 8.7 %collective-permute-start.9 = (f32[128,256]{1,0:T(8,128)S(1)}, f32[128,256]{1,0:T(8,128)S(1)}, u32[]{:S(2)}, u32[]{:S(2)}) collective-permute-start(f32[128,256]{1,0:T(8,128)S(1)} %get-tuple-element.18), channel_id=1, source_target_pairs={{0,2},{1,3},{2,0},{3,1},{4,6},{5,7},{6,4},{7,5},{8,10},{9,11},{10,... | collective-permute-start | bytes 393224 | tf_op jit(solution)/shard_map/ppermute | solution.py:279
  20.1 16.4 %collective-permute-start.8 = (f32[128,384]{1,0:T(8,128)S(1)}, f32[128,384]{1,0:T(8,128)S(1)}, u32[]{:S(2)}, u32[]{:S(2)}) collective-permute-start(f32[128,384]{1,0:T(8,128)S(1)} %get-tuple-element.17.refs_0_), channel_id=1, source_target_pairs={{0,1},{1,0},{2,3},{3,2},{4,5},{5,4},{6,7},{7,6},{8,9},{9,8},{10,11... | collective-permute-start | bytes 589832 | tf_op jit(solution)/shard_map/ppermute | solution.py:279
  21.5 8.2 %collective-permute-start.7 = (f32[128,256]{1,0:T(8,128)S(1)}, f32[128,256]{1,0:T(8,128)S(1)}, u32[]{:S(2)}, u32[]{:S(2)}) collective-permute-start(f32[128,256]{1,0:T(8,128)S(1)} %get-tuple-element.16), channel_id=1, source_target_pairs={{0,3},{1,2},{2,1},{3,0},{4,7},{5,6},{6,5},{7,4},{8,11},{9,10},{10,... | collective-permute-start | bytes 393224 | tf_op jit(solution)/shard_map/ppermute | solution.py:279
  22.8 26.1 %collective-permute-start.3 = (f32[128,512]{1,0:T(8,128)S(1)}, f32[128,512]{1,0:T(8,128)S(1)}, u32[]{:S(2)}, u32[]{:S(2)}) collective-permute-start(f32[128,512]{1,0:T(8,128)S(1)} %get-tuple-element.14.refs_0_), channel_id=1, source_target_pairs={{0,3},{1,2},{2,1},{3,0},{4,7},{5,6},{6,5},{7,4},{8,11},{9,10},{10,... | collective-permute-start | bytes 786440 | tf_op jit(solution)/shard_map/ppermute | solution.py:279
  24.5 24.4 %collective-permute-start.2 = (f32[128,512]{1,0:T(8,128)S(1)}, f32[128,512]{1,0:T(8,128)S(1)}, u32[]{:S(2)}, u32[]{:S(2)}) collective-permute-start(f32[128,512]{1,0:T(8,128)S(1)} %get-tuple-element.14.refs_0_), channel_id=1, source_target_pairs={{0,2},{1,3},{2,0},{3,1},{4,6},{5,7},{6,4},{7,5},{8,10},{9,11},{10,... | collective-permute-start | bytes 786440 | tf_op jit(solution)/shard_map/ppermute | solution.py:279
  26.5 22.4 %collective-permute-start.1 = (f32[128,512]{1,0:T(8,128)S(1)}, f32[128,512]{1,0:T(8,128)S(1)}, u32[]{:S(2)}, u32[]{:S(2)}) collective-permute-start(f32[128,512]{1,0:T(8,128)S(1)} %get-tuple-element.14.refs_0_), channel_id=1, source_target_pairs={{0,1},{1,0},{2,3},{3,2},{4,5},{5,4},{6,7},{7,6},{8,9},{9,8},{10,11... | collective-permute-start | bytes 786440 | tf_op jit(solution)/shard_map/ppermute | solution.py:279
  29.7 19.2 %collective-permute-start.5 = (f32[128,384]{1,0:T(8,128)S(1)}, f32[128,384]{1,0:T(8,128)S(1)}, u32[]{:S(2)}, u32[]{:S(2)}) collective-permute-start(f32[128,384]{1,0:T(8,128)S(1)} %get-tuple-element.15.refs_4_), channel_id=1, source_target_pairs={{0,1},{1,0},{2,3},{3,2},{4,5},{5,4},{6,7},{7,6},{8,9},{9,8},{10,11... | collective-permute-start | bytes 589832 | tf_op jit(solution)/shard_map/ppermute | solution.py:279
  36.5 12.3 %collective-permute-start.6 = (f32[128,256]{1,0:T(8,128)S(1)}, f32[128,256]{1,0:T(8,128)S(1)}, u32[]{:S(2)}, u32[]{:S(2)}) collective-permute-start(f32[128,256]{1,0:T(8,128)S(1)} %get-tuple-element.16), channel_id=1, source_target_pairs={{0,2},{1,3},{2,0},{3,1},{4,6},{5,7},{6,4},{7,5},{8,10},{9,11},{10,... | collective-permute-start | bytes 393224 | tf_op jit(solution)/shard_map/ppermute | solution.py:279
  63.4 8.7 %collective-permute-start.11 = (bf16[128,512]{1,0:T(8,128)(2,1)S(1)}, bf16[128,512]{1,0:T(8,128)(2,1)S(1)}, u32[]{:S(2)}, u32[]{:S(2)}) collective-permute-start(bf16[128,512]{1,0:T(8,128)(2,1)S(1)} %get-tuple-element.22), channel_id=1, source_target_pairs={{0,4},{1,5},{2,6},{3,7},{4,0},{5,1},{6,2},{7,3},{8,12},{9,13},{10,... | collective-permute-start | bytes 393224 | tf_op jit(solution)/shard_map/ppermute | solution.py:279
where the time goes:
time: 73.8 us; the launch traced here: 73.6 us
  Pallas kernels  30.2 us (41%)
  waiting for transfers between devices  24.7 us (33%)
  starting transfers between devices  16.4 us (22%)
  local copies, waits for them, and re-layouts  1.74 us (2%)
    pallas_call x4, Pallas kernels, local(): pl.pallas_call(kernel, out_shape=[pltpu.VMEM(*out) for out in outs], in_s...  28.8 us
    ppermute x12, waiting for transfers between devices, swap(): return lax.ppermute(shard, 'blk', [(i, i ^ by) for i in range(cycle_size)])  24.7 us
    ppermute x12, starting transfers between devices, swap(): return lax.ppermute(shard, 'blk', [(i, i ^ by) for i in range(cycle_size)])  16.4 us
  transfers between devices with their start and end apart: 12, of which 5 were waited for; matrix products, arithmetic and copies ran while one was open for 2% of the time, Pallas kernels for 19%

commit v1 on v0

--- a/solution.py
+++ b/solution.py
@@ -229,7 +229,7 @@
 def second_kernel(where, *refs):
     count = PANEL_WIDTH // BLOCK_WIDTH
     sides, fars = refs[:count], refs[count : 2 * count]
-    upper, inverse, mine, send, side, square, own_inverse = refs[2 * count :]
+    upper, inverse, out, keep, send, side, square, own_inverse, left_rows, done = refs[2 * count :]
     me, half = where[0], where[1]
     for m in range(count):
         side[block_rows(jnp.bitwise_xor(me, m)), :] = sides[m][...]
@@ -241,6 +241,13 @@
         solved = halves(value)
         for i in range(b + 1, count):
             side[i * BLOCK_WIDTH : (i + 1) * BLOCK_WIDTH, :] -= product3(halves(upper[i, rows, :].T), solved)
+    rows = block_rows(me)
+    for j in range(count):
+        kept = (j >= me) & (half == 0)
+        left_rows[:, block_lanes(j)] = jnp.where(kept, upper[j, rows, :], 0.0).astype(BF16).astype(F32)
+    copy = pltpu.make_async_copy(left_rows, out.at[:, :PANEL_WIDTH], done)
+    copy.start()
+    keep[...] = side[rows, :].astype(BF16).astype(F32)
     rounded = side[...].astype(BF16)
     for i in range(count):
         left = rounded[:, i * BLOCK_WIDTH : (i + 1) * BLOCK_WIDTH].T
@@ -250,20 +257,15 @@
                 :, (j - i) * BLOCK_WIDTH : (j - i + 1) * BLOCK_WIDTH
             ]
     factor_panel(square, own_inverse, sides[0][:SUBS, :LANES] * 0.0)
-    rows = block_rows(me)
     for j in range(count):
-        kept = (j >= me) & (half == 0)
-        mine[:, block_lanes(j)] = jnp.where(kept, upper[j, rows, :], 0.0).astype(BF16).astype(F32)
         send[:, block_lanes(j)] = jnp.where(j >= me, square[j, rows, :], 0.0).astype(BF16)
-    mine[:, PANEL_WIDTH:] = side[rows, :].astype(BF16).astype(F32)
-
-
-def finish_kernel(where, mine, got, out, done):
-    @pl.when(where[1] == 1)
-    def _():
-        mine[:, PANEL_WIDTH:] = got[...].astype(F32)
-
-    copy = pltpu.make_async_copy(mine, out, done)
+    copy.wait()
+
+
+def finish_kernel(where, begun, keep, got, out, wide, done):
+    del begun
+    wide[...] = jnp.where(where[1] == 1, got[...].astype(F32), keep[...])
+    copy = pltpu.make_async_copy(wide, out.at[:, PANEL_WIDTH:], done)
     copy.start()
     copy.wait()
 
@@ -291,6 +293,7 @@
 
     scalar = pl.BlockSpec(memory_space=pltpu.SMEM)
     vector = pl.BlockSpec(memory_space=pltpu.VMEM)
+    anywhere = pl.BlockSpec(memory_space=pl.ANY)
     where = jnp.stack([me, half]).astype(jnp.int32)
     square_shape = (count, PANEL_WIDTH, BLOCK_WIDTH)
     inverse_shape = (PANEL_WIDTH, BLOCK_WIDTH)
@@ -307,9 +310,9 @@
     def local(kernel, outs, ins, scratch=()):
         return pl.pallas_call(
             kernel,
-            out_shape=[pltpu.VMEM(*out) for out in outs],
+            out_shape=[out if isinstance(out, jax.ShapeDtypeStruct) else pltpu.VMEM(*out) for out in outs],
             in_specs=[scalar] + [vector] * len(ins),
-            out_specs=[vector] * len(outs),
+            out_specs=[anywhere if isinstance(out, jax.ShapeDtypeStruct) else vector for out in outs],
             scratch_shapes=scratch,
             compiler_params=grant,
         )(where, *[near(array) for array in ins])
@@ -336,26 +339,29 @@
     far, wide_far = local(far_kernel, [(diag_shape, F32), (wide_shape, F32)], [far, kids, far_hot, col_hot], [full])
     fars = share(far, wide_far)
     upper, inverse = local(first_kernel, [(square_shape, F32), (inverse_shape, F32)], diags)
-    mine, send = local(
+    begun, keep, send = local(
         second_kernel,
-        [((BLOCK_WIDTH, 2 * PANEL_WIDTH), F32), (side_shape, BF16)],
+        [jax.ShapeDtypeStruct((BLOCK_WIDTH, 2 * PANEL_WIDTH), F32), (side_shape, F32), (side_shape, BF16)],
         [*sides, *fars, upper, inverse],
         [
             pltpu.VMEM((PANEL_WIDTH, PANEL_WIDTH), F32),
             pltpu.VMEM(square_shape, F32),
             pltpu.VMEM(inverse_shape, F32),
+            pltpu.VMEM(side_shape, F32),
+            pltpu.SemaphoreType.DMA,
         ],
     )
     got = swap(send, count)
     result = pl.pallas_call(
         finish_kernel,
         out_shape=jax.ShapeDtypeStruct((BLOCK_WIDTH, 2 * PANEL_WIDTH), F32),
-        in_specs=[scalar, vector, vector],
-        out_specs=pl.BlockSpec(memory_space=pl.ANY),
-        scratch_shapes=[pltpu.SemaphoreType.DMA],
+        in_specs=[scalar, anywhere, vector, vector],
+        out_specs=anywhere,
+        input_output_aliases={1: 0},
+        scratch_shapes=[pltpu.VMEM(side_shape, F32), pltpu.SemaphoreType.DMA],
         compiler_params=grant,
         name="finish",
-    )(where, near(mine), near(got))
+    )(where, begun, near(keep), near(got))
     return result[None]
 
 

time: 73.8 us -> 74.4 us (level)
  no operation moved by 1% of the time
where the time goes in v1:
time: 74.4 us; the launch traced here: 74.2 us
  Pallas kernels  30.8 us (41%)
  waiting for transfers between devices  24.7 us (33%)
  starting transfers between devices  16.4 us (22%)
  local copies, waits for them, and re-layouts  1.74 us (2%)
    pallas_call x4, Pallas kernels, local(): pl.pallas_call(kernel, out_shape=[out if isinstance(out, jax.ShapeDtypeSt...  29.5 us
    ppermute x12, waiting for transfers between devices, swap(): return lax.ppermute(shard, 'blk', [(i, i ^ by) for i in range(cycle_size)])  24.7 us
    ppermute x12, starting transfers between devices, swap(): return lax.ppermute(shard, 'blk', [(i, i ^ by) for i in range(cycle_size)])  16.4 us
  transfers between devices with their start and end apart: 12, of which 5 were waited for; matrix products, arithmetic and copies ran while one was open for 2% of the time, Pallas kernels for 19%

profile of v1, /device:TPU:0, one launch (start us, length us, event | category | flops | bytes accessed | tf_op | source)
XLA Modules:
  0.0 74.2 jit_solution(17825523089637590407)
XLA Ops:
  0.0 4.1 %collective-permute-start = (f32[64,512]{1,0:T(8,128)}, f32[64,512]{1,0:T(8,128)S(1)}, u32[]{:S(2)}, u32[]{:S(2)}) collective-permute-start(f32[64,512]{1,0:T(8,128)} %bitcast.12), channel_id=1, source_target_pairs={{0,4},{1,5},{2,6},{3,7},{4,0},{5,1},{6,2},{7,3},{8,12},{9,13},{10,... | collective-permute-start | bytes 393224 | tf_op jit(solution)/shard_map/ppermute | solution.py:281
  4.1 1.0 %dynamic-slice_bitcast_fusion.2 = (f32[128,128]{1,0:T(8,128)S(1)}, f32[128,128]{1,0:T(8,128)S(1)}, f32[128,128]{1,0:T(8,128)S(1)}) fusion(f32[1,128,1024]{2,1,0:T(8,128)} %param.3, s32[]{:T(128)S(6)} %select_n.65, s32[]{:T(128)S(6)} %select_n.69, s32[]{:T(128)S(6)} %select_n.67), kind=kLoop, calls=%fused_computation.6 | loop fusion | bytes 393228 | tf_op jit(solution)/shard_map/dynamic_slice | solution.py:324
  5.2 0.7 copy-done.2
  5.9 0.1 fusion.col_hot
  6.2 9.5 %collective-permute-done.kids = f32[64,512]{1,0:T(8,128)S(1)} collective-permute-done((f32[64,512]{1,0:T(8,128)}, f32[64,512]{1,0:T(8,128)S(1)}, u32[]{:S(2)}, u32[]{:S(2)}) %collective-permute-start) | collective-permute-done | bytes 131104 | tf_op jit(solution)/shard_map/ppermute | solution.py:281
  15.6 1.1 %shard_map.37 = (f32[128,256]{1,0:T(8,128)S(1)}, f32[128,384]{1,0:T(8,128)S(1)}, f32[128,512]{1,0:T(8,128)S(1)}) custom-call(s32[2]{0:T(128)S(1)} %pad_add_fusion.where, f32[128,1024]{1,0:T(8,128)S(1)} %bitcast.11, f32[64,512]{1,0:T(8,128)S(1)} %collective-permute-done.kids, bf16[128,64]{1,0:T(8,128)(2,1)S(1)} %fusion.1.row_hot, ...), custom_call_target="tpu_custom_call" | custom-call | tf_op jit(solution)/shard_map/pallas_call | solution.py:311
  16.8 1.1 %collective-permute-start.10 = (f32[128,256]{1,0:T(8,128)S(1)}, f32[128,256]{1,0:T(8,128)S(1)}, u32[]{:S(2)}, u32[]{:S(2)}) collective-permute-start(f32[128,256]{1,0:T(8,128)S(1)} %get-tuple-element.19), channel_id=1, source_target_pairs={{0,3},{1,2},{2,1},{3,0},{4,7},{5,6},{6,5},{7,4},{8,11},{9,10},{10,... | collective-permute-start | bytes 393224 | tf_op jit(solution)/shard_map/ppermute | solution.py:281
  17.8 2.3 %collective-permute-start.9 = (f32[128,256]{1,0:T(8,128)S(1)}, f32[128,256]{1,0:T(8,128)S(1)}, u32[]{:S(2)}, u32[]{:S(2)}) collective-permute-start(f32[128,256]{1,0:T(8,128)S(1)} %get-tuple-element.19), channel_id=1, source_target_pairs={{0,2},{1,3},{2,0},{3,1},{4,6},{5,7},{6,4},{7,5},{8,10},{9,11},{10,... | collective-permute-start | bytes 393224 | tf_op jit(solution)/shard_map/ppermute | solution.py:281
  20.1 0.3 collective-permute-start.8
  20.4 1.1 %shard_map.38 = (f32[128,256]{1,0:T(8,128)S(1)}, f32[128,384]{1,0:T(8,128)S(1)}) custom-call(s32[2]{0:T(128)S(1)} %pad_add_fusion.where, f32[128,384]{1,0:T(8,128)S(1)} %collective-permute-done.4.raw, f32[64,512]{1,0:T(8,128)S(1)} %bitcast.13, bf16[128,64]{1,0:T(8,128)(2,1)S(1)} %fusion.2.row_hot, bf16[512,256]{1,0:T(8,128)(2,1)S(1)} %fusion.col_hot), custom_call_target="tpu_custom_call" | custom-call | tf_op jit(solution)/shard_map/pallas_call | solution.py:311
  21.5 1.3 %collective-permute-start.7 = (f32[128,256]{1,0:T(8,128)S(1)}, f32[128,256]{1,0:T(8,128)S(1)}, u32[]{:S(2)}, u32[]{:S(2)}) collective-permute-start(f32[128,256]{1,0:T(8,128)S(1)} %get-tuple-element.17), channel_id=1, source_target_pairs={{0,3},{1,2},{2,1},{3,0},{4,7},{5,6},{6,5},{7,4},{8,11},{9,10},{10,... | collective-permute-start | bytes 393224 | tf_op jit(solution)/shard_map/ppermute | solution.py:281
  22.8 1.7 %collective-permute-start.3 = (f32[128,512]{1,0:T(8,128)S(1)}, f32[128,512]{1,0:T(8,128)S(1)}, u32[]{:S(2)}, u32[]{:S(2)}) collective-permute-start(f32[128,512]{1,0:T(8,128)S(1)} %get-tuple-element.15.refs_0_), channel_id=1, source_target_pairs={{0,3},{1,2},{2,1},{3,0},{4,7},{5,6},{6,5},{7,4},{8,11},{9,10},{10,... | collective-permute-start | bytes 786440 | tf_op jit(solution)/shard_map/ppermute | solution.py:281
  24.5 0.4 collective-permute-start.2
  24.9 1.7 %collective-permute-done.9.refs_2_ = f32[128,256]{1,0:T(8,128)S(1)} collective-permute-done((f32[128,256]{1,0:T(8,128)S(1)}, f32[128,256]{1,0:T(8,128)S(1)}, u32[]{:S(2)}, u32[]{:S(2)}) %collective-permute-start.9) | collective-permute-done | bytes 131104 | tf_op jit(solution)/shard_map/ppermute | solution.py:281
  26.5 0.9 %collective-permute-start.1 = (f32[128,512]{1,0:T(8,128)S(1)}, f32[128,512]{1,0:T(8,128)S(1)}, u32[]{:S(2)}, u32[]{:S(2)}) collective-permute-start(f32[128,512]{1,0:T(8,128)S(1)} %get-tuple-element.15.refs_0_), channel_id=1, source_target_pairs={{0,1},{1,0},{2,3},{3,2},{4,5},{5,4},{6,7},{7,6},{8,9},{9,8},{10,11... | collective-permute-start | bytes 786440 | tf_op jit(solution)/shard_map/ppermute | solution.py:281
  27.5 2.2 %collective-permute-done.7.refs_7_ = f32[128,256]{1,0:T(8,128)S(1)} collective-permute-done((f32[128,256]{1,0:T(8,128)S(1)}, f32[128,256]{1,0:T(8,128)S(1)}, u32[]{:S(2)}, u32[]{:S(2)}) %collective-permute-start.7) | collective-permute-done | bytes 131104 | tf_op jit(solution)/shard_map/ppermute | solution.py:281
  29.7 1.1 %collective-permute-start.5 = (f32[128,384]{1,0:T(8,128)S(1)}, f32[128,384]{1,0:T(8,128)S(1)}, u32[]{:S(2)}, u32[]{:S(2)}) collective-permute-start(f32[128,384]{1,0:T(8,128)S(1)} %get-tuple-element.16.refs_4_), channel_id=1, source_target_pairs={{0,1},{1,0},{2,3},{3,2},{4,5},{5,4},{6,7},{7,6},{8,9},{9,8},{10,11... | collective-permute-start | bytes 589832 | tf_op jit(solution)/shard_map/ppermute | solution.py:281
  30.8 5.7 %collective-permute-done.8.refs_1_ = f32[128,384]{1,0:T(8,128)S(1)} collective-permute-done((f32[128,384]{1,0:T(8,128)S(1)}, f32[128,384]{1,0:T(8,128)S(1)}, u32[]{:S(2)}, u32[]{:S(2)}) %collective-permute-start.8) | collective-permute-done | bytes 196640 | tf_op jit(solution)/shard_map/ppermute | solution.py:281
  36.5 0.2 collective-permute-start.6
  36.7 12.2 %shard_map.39 = (f32[4,512,128]{2,1,0:T(8,128)S(1)}, f32[512,128]{1,0:T(8,128)S(1)}) custom-call(s32[2]{0:T(128)S(1)} %pad_add_fusion.where, f32[128,384]{1,0:T(8,128)S(1)} %get-tuple-element.18.refs_0_, f32[128,384]{1,0:T(8,128)S(1)} %collective-permute-done.8.refs_1_, f32[128,256]{1,0:T(8,128)S(1)} %collective-permute-done.9.refs_2_, ...), custom_call_target="tpu_custom_call" | custom-call | tf_op jit(solution)/shard_map/pallas_call | solution.py:311
  48.9 15.2 %shard_map.40 = (f32[128,1024]{1,0:T(8,128)}, f32[128,512]{1,0:T(8,128)S(1)}, bf16[128,512]{1,0:T(8,128)(2,1)S(1)}) custom-call(s32[2]{0:T(128)S(1)} %pad_add_fusion.where, f32[128,512]{1,0:T(8,128)S(1)} %get-tuple-element.15.refs_0_, f32[128,512]{1,0:T(8,128)S(1)} %collective-permute-done.1.refs_1_, f32[128,512]{1,0:T(8,128)S(1)} %collective-permute-done.2.refs_2_, ...), custom_call_target="tpu_custom_call" | custom-call | tf_op jit(solution)/shard_map/pallas_call | solution.py:311
  64.1 3.1 %collective-permute-start.11 = (bf16[128,512]{1,0:T(8,128)(2,1)S(1)}, bf16[128,512]{1,0:T(8,128)(2,1)S(1)}, u32[]{:S(2)}, u32[]{:S(2)}) collective-permute-start(bf16[128,512]{1,0:T(8,128)(2,1)S(1)} %get-tuple-element.24), channel_id=1, source_target_pairs={{0,4},{1,5},{2,6},{3,7},{4,0},{5,1},{6,2},{7,3},{8,12},{9,13},{10,... | collective-permute-start | bytes 393224 | tf_op jit(solution)/shard_map/ppermute | solution.py:281
  67.2 5.6 %collective-permute-done.11.got = bf16[128,512]{1,0:T(8,128)(2,1)S(1)} collective-permute-done((bf16[128,512]{1,0:T(8,128)(2,1)S(1)}, bf16[128,512]{1,0:T(8,128)(2,1)S(1)}, u32[]{:S(2)}, u32[]{:S(2)}) %collective-permute-start.11) | collective-permute-done | bytes 131104 | tf_op jit(solution)/shard_map/ppermute | solution.py:281
  72.8 1.3 %finish.1 = f32[128,1024]{1,0:T(8,128)} custom-call(s32[2]{0:T(128)S(1)} %pad_add_fusion.where, f32[128,1024]{1,0:T(8,128)} %get-tuple-element.22.begun, f32[128,512]{1,0:T(8,128)S(1)} %get-tuple-element.23.keep, bf16[128,512]{1,0:T(8,128)(2,1)S(1)} %collective-permute-done.11.got), custom_call_target="tpu_custom_call", output_to_operand_aliasing={{}: (1, {})} | custom-call | tf_op jit(solution)/shard_map/finish/pallas_call | solution.py:355
  (19 shorter events, 0.3 us)
Async XLA Ops:
  0.0 15.6 %collective-permute-start = (f32[64,512]{1,0:T(8,128)}, f32[64,512]{1,0:T(8,128)S(1)}, u32[]{:S(2)}, u32[]{:S(2)}) collective-permute-start(f32[64,512]{1,0:T(8,128)} %bitcast.12), channel_id=1, source_target_pairs={{0,4},{1,5},{2,6},{3,7},{4,0},{5,1},{6,2},{7,3},{8,12},{9,13},{10,... | collective-permute-start | bytes 393224 | tf_op jit(solution)/shard_map/ppermute | solution.py:281
  4.1 11.6 %copy-start = (f32[1,128,1024]{2,1,0:T(8,128)S(1)}, f32[1,128,1024]{2,1,0:T(8,128)}, u32[]{:S(2)}) copy-start(f32[1,128,1024]{2,1,0:T(8,128)} %param.3) | copy-start | bytes 1572868
  5.1 15.3 %collective-permute-start.4 = (f32[128,384]{1,0:T(8,128)S(1)}, f32[128,384]{1,0:T(8,128)S(1)}, u32[]{:S(2)}, u32[]{:S(2)}) collective-permute-start(f32[128,384]{1,0:T(8,128)S(1)} %pad_maximum_fusion), channel_id=1, source_target_pairs={{0,4},{1,5},{2,6},{3,7},{4,0},{5,1},{6,2},{7,3},{8,12},{9,13},{10,... | collective-permute-start | bytes 589832 | tf_op jit(solution)/shard_map/ppermute | solution.py:281
  5.2 0.7 copy-start.2
  15.6 4.8 %copy-start.1 = (f32[1,64,512]{2,1,0:T(8,128)S(1)}, f32[1,64,512]{2,1,0:T(8,128)}, u32[]{:S(2)}) copy-start(f32[1,64,512]{2,1,0:T(8,128)} %param.4) | copy-start | bytes 393220
  16.8 7.7 %collective-permute-start.10 = (f32[128,256]{1,0:T(8,128)S(1)}, f32[128,256]{1,0:T(8,128)S(1)}, u32[]{:S(2)}, u32[]{:S(2)}) collective-permute-start(f32[128,256]{1,0:T(8,128)S(1)} %get-tuple-element.19), channel_id=1, source_target_pairs={{0,3},{1,2},{2,1},{3,0},{4,7},{5,6},{6,5},{7,4},{8,11},{9,10},{10,... | collective-permute-start | bytes 393224 | tf_op jit(solution)/shard_map/ppermute | solution.py:281
  17.8 8.7 %collective-permute-start.9 = (f32[128,256]{1,0:T(8,128)S(1)}, f32[128,256]{1,0:T(8,128)S(1)}, u32[]{:S(2)}, u32[]{:S(2)}) collective-permute-start(f32[128,256]{1,0:T(8,128)S(1)} %get-tuple-element.19), channel_id=1, source_target_pairs={{0,2},{1,3},{2,0},{3,1},{4,6},{5,7},{6,4},{7,5},{8,10},{9,11},{10,... | collective-permute-start | bytes 393224 | tf_op jit(solution)/shard_map/ppermute | solution.py:281
  20.1 16.4 %collective-permute-start.8 = (f32[128,384]{1,0:T(8,128)S(1)}, f32[128,384]{1,0:T(8,128)S(1)}, u32[]{:S(2)}, u32[]{:S(2)}) collective-permute-start(f32[128,384]{1,0:T(8,128)S(1)} %get-tuple-element.18.refs_0_), channel_id=1, source_target_pairs={{0,1},{1,0},{2,3},{3,2},{4,5},{5,4},{6,7},{7,6},{8,9},{9,8},{10,11... | collective-permute-start | bytes 589832 | tf_op jit(solution)/shard_map/ppermute | solution.py:281
  21.5 8.2 %collective-permute-start.7 = (f32[128,256]{1,0:T(8,128)S(1)}, f32[128,256]{1,0:T(8,128)S(1)}, u32[]{:S(2)}, u32[]{:S(2)}) collective-permute-start(f32[128,256]{1,0:T(8,128)S(1)} %get-tuple-element.17), channel_id=1, source_target_pairs={{0,3},{1,2},{2,1},{3,0},{4,7},{5,6},{6,5},{7,4},{8,11},{9,10},{10,... | collective-permute-start | bytes 393224 | tf_op jit(solution)/shard_map/ppermute | solution.py:281
  22.8 26.1 %collective-permute-start.3 = (f32[128,512]{1,0:T(8,128)S(1)}, f32[128,512]{1,0:T(8,128)S(1)}, u32[]{:S(2)}, u32[]{:S(2)}) collective-permute-start(f32[128,512]{1,0:T(8,128)S(1)} %get-tuple-element.15.refs_0_), channel_id=1, source_target_pairs={{0,3},{1,2},{2,1},{3,0},{4,7},{5,6},{6,5},{7,4},{8,11},{9,10},{10,... | collective-permute-start | bytes 786440 | tf_op jit(solution)/shard_map/ppermute | solution.py:281
  24.5 24.4 %collective-permute-start.2 = (f32[128,512]{1,0:T(8,128)S(1)}, f32[128,512]{1,0:T(8,128)S(1)}, u32[]{:S(2)}, u32[]{:S(2)}) collective-permute-start(f32[128,512]{1,0:T(8,128)S(1)} %get-tuple-element.15.refs_0_), channel_id=1, source_target_pairs={{0,2},{1,3},{2,0},{3,1},{4,6},{5,7},{6,4},{7,5},{8,10},{9,11},{10,... | collective-permute-start | bytes 786440 | tf_op jit(solution)/shard_map/ppermute | solution.py:281
  26.5 22.4 %collective-permute-start.1 = (f32[128,512]{1,0:T(8,128)S(1)}, f32[128,512]{1,0:T(8,128)S(1)}, u32[]{:S(2)}, u32[]{:S(2)}) collective-permute-start(f32[128,512]{1,0:T(8,128)S(1)} %get-tuple-element.15.refs_0_), channel_id=1, source_target_pairs={{0,1},{1,0},{2,3},{3,2},{4,5},{5,4},{6,7},{7,6},{8,9},{9,8},{10,11... | collective-permute-start | bytes 786440 | tf_op jit(solution)/shard_map/ppermute | solution.py:281
  29.7 19.2 %collective-permute-start.5 = (f32[128,384]{1,0:T(8,128)S(1)}, f32[128,384]{1,0:T(8,128)S(1)}, u32[]{:S(2)}, u32[]{:S(2)}) collective-permute-start(f32[128,384]{1,0:T(8,128)S(1)} %get-tuple-element.16.refs_4_), channel_id=1, source_target_pairs={{0,1},{1,0},{2,3},{3,2},{4,5},{5,4},{6,7},{7,6},{8,9},{9,8},{10,11... | collective-permute-start | bytes 589832 | tf_op jit(solution)/shard_map/ppermute | solution.py:281
  36.5 12.3 %collective-permute-start.6 = (f32[128,256]{1,0:T(8,128)S(1)}, f32[128,256]{1,0:T(8,128)S(1)}, u32[]{:S(2)}, u32[]{:S(2)}) collective-permute-start(f32[128,256]{1,0:T(8,128)S(1)} %get-tuple-element.17), channel_id=1, source_target_pairs={{0,2},{1,3},{2,0},{3,1},{4,6},{5,7},{6,4},{7,5},{8,10},{9,11},{10,... | collective-permute-start | bytes 393224 | tf_op jit(solution)/shard_map/ppermute | solution.py:281
  64.1 8.7 %collective-permute-start.11 = (bf16[128,512]{1,0:T(8,128)(2,1)S(1)}, bf16[128,512]{1,0:T(8,128)(2,1)S(1)}, u32[]{:S(2)}, u32[]{:S(2)}) collective-permute-start(bf16[128,512]{1,0:T(8,128)(2,1)S(1)} %get-tuple-element.24), channel_id=1, source_target_pairs={{0,4},{1,5},{2,6},{3,7},{4,0},{5,1},{6,2},{7,3},{8,12},{9,13},{10,... | collective-permute-start | bytes 393224 | tf_op jit(solution)/shard_map/ppermute | solution.py:281
